TPU v7x, 32 devices: a whole 2x2x4 slice. The times are simulated.
32 devices in a mesh: gx: 4 (over x, core), gy: 8 (over z, y).
Axes of the slice: x: 2, y: 2, z: 4, core: 2. Of those that a mesh axis runs over, the one named last changes fastest.
Arguments:
- mask_feats: bfloat16 [64, 8, 14, 14, 256], P(('gx', 'gy')), may hold values from -6 to 6
- mask_cot: bfloat16 [64, 8, 14, 14, 256], P(('gx', 'gy')), may hold values from -6 to 6
- roi_counts: int32 [64], P(('gx', 'gy')), may hold values from 1 to 8, as said below
- rpn_feats: bfloat16 [64, 48, 32, 256], P(('gx', 'gy')), may hold values from -6 to 6
- rpn_cot: bfloat16 [64, 48, 32, 256], P(('gx', 'gy')), may hold values from -360 to 360
- anchor_counts: int32 [64], P(('gx', 'gy')), may hold values from 32 to 223
- mask_weight: float32 [2304, 256], replicated, may hold values from -0.125 to 0.125
- rpn_weight: float32 [2304, 256], replicated, may hold values from -0.125 to 0.125
- mask_moment: float32 [2304, 256], replicated, may hold values from -6 to 6
- rpn_moment: float32 [2304, 256], replicated, may hold values from -6 to 6
Outputs:
- new_mask_weight: float32 [2304, 256], replicated
- new_rpn_weight: float32 [2304, 256], replicated
- new_mask_moment: float32 [2304, 256], replicated
- new_rpn_moment: float32 [2304, 256], replicated
Inputs may be any that keep to these rules, and one draw needn't show every extreme that they name: `roi_counts`: every image has at least one positive ROI; some image has all 8 slots positive.
All inputs are finite; a program needn't handle non-finite values.
Results may differ from a plain program's by a relative error of at most 0.0003.
Values sent between devices are 32-bit elements; how exact they have to be, the bound alone decides.
A program may use at most 128 MiB of HBM per device.

v0:
```python
import jax
import jax.numpy as jnp
from jax import lax
from jax.sharding import PartitionSpec as P


def weight_grad(feats, cotan):
    grid_rows = feats.shape[1]
    grid_cols = feats.shape[2]
    chans = feats.shape[3]
    padded = jnp.pad(feats, ((0, 0), (1, 1), (1, 1), (0, 0)))
    flat_cot = cotan.reshape(-1, chans)
    blocks = []
    for row_tap in range(3):
        for col_tap in range(3):
            window = padded[
                :, row_tap : row_tap + grid_rows, col_tap : col_tap + grid_cols, :
            ].reshape(-1, chans)
            blocks.append(
                lax.dot_general(
                    window, flat_cot, (((0,), (0,)), ((), ())), preferred_element_type=jnp.float32
                )
            )
    return jnp.concatenate(blocks, axis=0)


def step_update(weight, moment, grad):
    fresh_moment = 0.9 * moment + grad
    return (weight - 0.02 * fresh_moment, fresh_moment)


def on_device(
    mask_feats,
    mask_cot,
    roi_counts,
    rpn_feats,
    rpn_cot,
    anchor_counts,
    mask_weight,
    rpn_weight,
    mask_moment,
    rpn_moment,
):
    slot_count = mask_feats.shape[1]
    side = mask_feats.shape[2]
    chans = mask_feats.shape[4]
    slots = jnp.arange(slot_count, dtype=jnp.int32)
    valid_slots = (slots[None, :] < roi_counts[:, None]).astype(jnp.bfloat16)
    masked = mask_cot * valid_slots[:, :, None, None, None]
    mask_local = weight_grad(
        mask_feats.reshape(-1, side, side, chans), masked.reshape(-1, side, side, chans)
    )
    rpn_local = weight_grad(rpn_feats, rpn_cot)
    local_counts = jnp.stack([jnp.sum(roi_counts), jnp.sum(anchor_counts)]).astype(jnp.float32)
    mask_sum, rpn_sum, totals = lax.psum((mask_local, rpn_local, local_counts), ("gx", "gy"))
    mask_grad = mask_sum / totals[0]
    rpn_grad = rpn_sum / totals[1]
    new_mask_weight, new_mask_moment = step_update(mask_weight, mask_moment, mask_grad)
    new_rpn_weight, new_rpn_moment = step_update(rpn_weight, rpn_moment, rpn_grad)
    return (new_mask_weight, new_rpn_weight, new_mask_moment, new_rpn_moment)


def solution(mesh):
    placed = (
        P(("gx", "gy"), None, None, None, None),
        P(("gx", "gy"), None, None, None, None),
        P(("gx", "gy")),
        P(("gx", "gy"), None, None, None),
        P(("gx", "gy"), None, None, None),
        P(("gx", "gy")),
        P(),
        P(),
        P(),
        P(),
    )
    return jax.shard_map(
        on_device, mesh=mesh, in_specs=placed, out_specs=(P(), P(), P(), P()), check_vma=False
    )
```

profile of v0, /device:TPU:0, one launch (start us, length us, event | category | flops | bytes accessed | tf_op | source)
XLA Modules:
  0.0 258.9 jit_solution(18293968853926520437)
XLA Ops:
  8.1 1.6 broadcast_multiply_fusion
  9.7 1.6 copy.29
  11.3 3.7 %reshape_reshape.3 = bf16[3136,256]{1,0:T(8,128)(2,1)} reshape(bf16[2,8,14,14,256]{4,3,2,1,0:T(8,128)(2,1)} %copy.29) | data formatting | bytes 3211264 | tf_op jit(solution)/shard_map/reshape;reshape | solution.py:12
  15.0 1.6 copy.81
  16.5 4.3 %pad_slice_fusion = (bf16[16,14,14,256]{3,0,2,1:T(8,128)(2,1)}, bf16[16,14,14,256]{3,0,2,1:T(8,128)(2,1)}, bf16[16,14,14,256]{3,0,2,1:T(8,128)(2,1)}, bf16[16,14...) fusion(bf16[16,14,14,256]{3,0,2,1:T(8,128)(2,1)S(1)} %bitcast.89), kind=kLoop, calls=%fused_computation.4 | loop fusion | bytes 14450688 | tf_op jit(solution)/shard_map/slice | solution.py:16
  20.8 1.8 copy.28
  22.7 3.6 %reshape.70 = bf16[3136,256]{1,0:T(8,128)(2,1)} reshape(bf16[16,14,14,256]{3,2,1,0:T(8,128)(2,1)} %copy.28) | data formatting | bytes 3211264 | tf_op jit(solution)/shard_map/reshape | solution.py:18
  26.3 3.3 %copy.30 = bf16[16,14,14,256]{3,2,1,0:T(8,128)(2,1)} copy(bf16[16,14,14,256]{3,0,2,1:T(8,128)(2,1)} %get-tuple-element.11) | data formatting | bytes 3211264 | tf_op jit(solution)/shard_map/slice | solution.py:16
  29.6 3.6 %reshape.71 = bf16[3136,256]{1,0:T(8,128)(2,1)} reshape(bf16[16,14,14,256]{3,2,1,0:T(8,128)(2,1)} %copy.30) | data formatting | bytes 3211264 | tf_op jit(solution)/shard_map/reshape | solution.py:18
  33.2 3.3 %copy.31 = bf16[16,14,14,256]{3,2,1,0:T(8,128)(2,1)} copy(bf16[16,14,14,256]{3,0,2,1:T(8,128)(2,1)} %get-tuple-element.12) | data formatting | bytes 3211264 | tf_op jit(solution)/shard_map/slice | solution.py:16
  36.5 3.6 %reshape.72 = bf16[3136,256]{1,0:T(8,128)(2,1)} reshape(bf16[16,14,14,256]{3,2,1,0:T(8,128)(2,1)} %copy.31) | data formatting | bytes 3211264 | tf_op jit(solution)/shard_map/reshape | solution.py:18
  40.1 3.3 %copy.32 = bf16[16,14,14,256]{3,2,1,0:T(8,128)(2,1)} copy(bf16[16,14,14,256]{3,0,2,1:T(8,128)(2,1)} %get-tuple-element.13) | data formatting | bytes 3211264 | tf_op jit(solution)/shard_map/slice | solution.py:16
  43.3 3.6 %reshape.73 = bf16[3136,256]{1,0:T(8,128)(2,1)} reshape(bf16[16,14,14,256]{3,2,1,0:T(8,128)(2,1)} %copy.32) | data formatting | bytes 3211264 | tf_op jit(solution)/shard_map/reshape | solution.py:18
  47.0 3.4 %convolution_dynamic-update-slice_fusion.7 = f32[2304,256]{1,0:T(8,128)} fusion(bf16[3136,256]{1,0:T(8,128)(2,1)} %reshape.70, bf16[3136,256]{1,0:T(8,128)(2,1)} %reshape_reshape.3), kind=kOutput, calls=%fused_computation.36 | convolution fusion | flops 411041792 | bytes 3473408 | tf_op jit(solution)/shard_map/dot_general | solution.py:20
  54.7 1.5 fusion.25
  56.8 1.4 reshape.74
  58.2 2.0 copy.36
  60.2 1.4 reshape.75
  61.6 2.0 copy.37
  63.6 1.4 reshape.76
  65.0 2.0 copy.38
  67.1 1.4 reshape.77
  68.5 2.3 copy.39
  70.8 1.8 fusion.24
  72.6 2.1 fusion.22
  74.7 2.0 fusion.20
  80.1 2.1 fusion.14
  82.2 2.3 fusion.12
  84.5 2.1 fusion.10
  96.5 42.4 %psum.22 = f32[2]{0:T(128)S(1)} all-reduce(f32[2]{0:T(128)S(1)} %add_convert_fusion), channel_id=1, replica_groups=mesh['gx'=4,'gy'=8] {'gx','gy'}, use_global_device_ids=true, to_apply=%region_3.4 | all-reduce | flops 2 | bytes 16 | tf_op jit(solution)/shard_map/psum | solution.py:55
  139.5 101.9 %all-reduce.5.cloned.1.call-done = (f32[2304,256]{1,0:T(8,128)}, f32[2304,256]{1,0:T(8,128)}) async-done(((f32[2304,256]{1,0:T(8,128)}, f32[2304,256]{1,0:T(8,128)}), (f32[2304,256]{1,0:T(8,128)}, f32[2304,256]{1,0:T(8,128)})) %all-reduce.5.cloned.1.call-update) | async-done | bytes 4718608 | tf_op jit(solution)/shard_map/psum | solution.py:55
  241.5 10.6 %multiply_subtract_fusion = (f32[2304,256]{1,0:T(8,128)}, f32[2304,256]{1,0:T(8,128)}, f32[2304,256]{1,0:T(8,128)}, f32[2304,256]{1,0:T(8,128)}) fusion(f32[2304,256]{1,0:T(8,128)} %param.17, f32[2304,256]{1,0:T(8,128)} %get-tuple-element.5, f32[]{:T(128)} %bitcast.25, f32[2304,256]{1,0:T(8,128)} %param.19, f32[2304,256]{1,0:T(8,128)} %param.16, ...), kind=kLoop, calls=%fused_computation | loop fusion | flops 5898240 | bytes 23592968 | tf_op jit(solution)/shard_map/sub | solution.py:29
  (50 shorter events, 19.6 us)
Async XLA Ops:
  7.2 63.6 %copy-start = (bf16[2,48,32,256]{3,2,1,0:T(8,128)(2,1)S(1)}, bf16[2,48,32,256]{3,2,1,0:T(8,128)(2,1)}, u32[]{:S(2)}) copy-start(bf16[2,48,32,256]{3,2,1,0:T(8,128)(2,1)} %param.14) | copy-start | bytes 4718596
  7.2 234.3 %all-reduce.5.cloned.1.call-start = ((), (), s32[]{:S(2)}) async-start(), calls=%async_computation | async-start | bytes 9437184 | tf_op jit(solution)/shard_map/psum | solution.py:55
  47.0 3.4 %copy-start.5 = (bf16[3136,256]{1,0:T(8,128)(2,1)S(1)}, bf16[3136,256]{1,0:T(8,128)(2,1)}, u32[]{:S(2)}) copy-start(bf16[3136,256]{1,0:T(8,128)(2,1)} %reshape_reshape.3) | copy-start | bytes 4816900
  47.0 3.4 %copy-start.11 = (bf16[3136,256]{1,0:T(8,128)(2,1)S(1)}, bf16[3136,256]{1,0:T(8,128)(2,1)}, u32[]{:S(2)}) copy-start(bf16[3136,256]{1,0:T(8,128)(2,1)} %reshape.71) | copy-start | bytes 4816900
  50.4 1.4 copy-start.12
  51.8 1.4 copy-start.13
  53.2 1.4 copy-start.2
  54.7 1.5 copy-start.1
  76.7 1.4 copy-start.3
  84.5 2.1 copy-start.6
  84.5 2.1 copy-start.7
  86.6 1.5 copy-start.4
  86.6 2.4 copy-start.8
  89.0 1.4 copy-start.9
  90.4 1.4 copy-start.10
  93.2 0.7 copy-start.14
  93.2 1.3 copy-start.15
Sparse Core Ops, SparseCore 0:
  93.3 148.0 all-reduce.4
where the time goes:
time: 260 us; the launch traced here: 259 us
  waiting for transfers between devices  102 us (39%)
  local copies, waits for them, and re-layouts  54.6 us (21%)
  blocking collectives  42.4 us (16%)
  matrix products  30 us (12%)
  other arithmetic  15.6 us (6%)
  between operations  14.2 us (5%)
    psum x1, waiting for transfers between devices, on_device(): lax.psum((mask_local, rpn_local, local_counts), ('gx', 'gy'))  102 us
    psum x1, blocking collectives, on_device(): lax.psum((mask_local, rpn_local, local_counts), ('gx', 'gy'))  42.4 us
    dot_general x18, matrix products, weight_grad(): lax.dot_general(window, flat_cot, (((0,), (0,)), ((), ())), preferred_ele...  30 us
    slice x9, local copies, waits for them, and re-layouts, weight_grad(): padded[:, row_tap:row_tap + grid_rows, col_tap:col_tap + grid_cols, :]  22.6 us
    reshape x8, local copies, waits for them, and re-layouts, weight_grad(): window = padded[:, row_tap:row_tap + grid_rows, col_tap:col_tap + grid_co...  20.2 us
    sub x1, other arithmetic, step_update(): return (weight - 0.02 * fresh_moment, fresh_moment)  10.6 us
    unnamed x34, local copies, waits for them, and re-layouts  5.92 us
  transfers between devices with their start and end apart: 1, of which 1 were waited for; matrix products, arithmetic and copies ran while one was open for 1% of the time, Pallas kernels for 0%

commit v1 on v0

--- a/solution.py
+++ b/solution.py
@@ -52,7 +52,9 @@
     )
     rpn_local = weight_grad(rpn_feats, rpn_cot)
     local_counts = jnp.stack([jnp.sum(roi_counts), jnp.sum(anchor_counts)]).astype(jnp.float32)
-    mask_sum, rpn_sum, totals = lax.psum((mask_local, rpn_local, local_counts), ("gx", "gy"))
+    mask_sum, rpn_sum, totals = lax.psum(
+        lax.psum((mask_local, rpn_local, local_counts), "gy"), "gx"
+    )
     mask_grad = mask_sum / totals[0]
     rpn_grad = rpn_sum / totals[1]
     new_mask_weight, new_mask_moment = step_update(mask_weight, mask_moment, mask_grad)

time: 260 us -> 380 us (1.46)
  waiting for transfers between devices: 102 us -> 238 us
  blocking collectives: 42.4 us -> 25.8 us
    psum x1 -> x2, waiting for transfers between devices: 102 us -> 238 us  [the longest x1 172 us: on_device(): lax.psum((mask_local, rpn_local, local_counts), 'gy')]
    psum x1 -> x2, blocking collectives: 42.4 us -> 25.8 us  [the longest x1 19.3 us: on_device(): lax.psum((mask_local, rpn_local, local_counts), 'gy')]
  transfers between devices with their start and end apart: 1 -> 2, of which waited for: 1 -> 2; matrix products, arithmetic and copies ran while one was open for 1% -> 1% of each run, Pallas kernels for 0% -> 0%
where the time goes in v1:
time: 380 us; the launch traced here: 379 us
  waiting for transfers between devices  238 us (63%)
  local copies, waits for them, and re-layouts  54.6 us (14%)
  matrix products  30 us (8%)
  blocking collectives  25.8 us (7%)
  other arithmetic  15.6 us (4%)
  between operations  14.2 us (4%)
    psum x1, waiting for transfers between devices, on_device(): lax.psum((mask_local, rpn_local, local_counts), 'gy')  172 us
    psum x1, waiting for transfers between devices, on_device(): lax.psum(lax.psum((mask_local, rpn_local, local_counts), 'gy'), 'gx')  65.9 us
    dot_general x18, matrix products, weight_grad(): lax.dot_general(window, flat_cot, (((0,), (0,)), ((), ())), preferred_ele...  30 us
    slice x9, local copies, waits for them, and re-layouts, weight_grad(): padded[:, row_tap:row_tap + grid_rows, col_tap:col_tap + grid_cols, :]  22.6 us
    reshape x8, local copies, waits for them, and re-layouts, weight_grad(): window = padded[:, row_tap:row_tap + grid_rows, col_tap:col_tap + grid_co...  20.1 us
    psum x1, blocking collectives, on_device(): lax.psum((mask_local, rpn_local, local_counts), 'gy')  19.3 us
    sub x1, other arithmetic, step_update(): return (weight - 0.02 * fresh_moment, fresh_moment)  10.5 us
  transfers between devices with their start and end apart: 2, of which 2 were waited for; matrix products, arithmetic and copies ran while one was open for 1% of the time, Pallas kernels for 0%

profile of v1, /device:TPU:0, one launch (start us, length us, event | category | flops | bytes accessed | tf_op | source)
XLA Modules:
  0.0 378.6 jit_solution(16341040553515071347)
XLA Ops:
  8.1 1.6 broadcast_multiply_fusion
  9.7 1.6 copy.29
  11.3 3.7 reshape_reshape.3
  15.0 1.6 copy.81
  16.5 4.3 %pad_slice_fusion = (bf16[16,14,14,256]{3,0,2,1:T(8,128)(2,1)}, bf16[16,14,14,256]{3,0,2,1:T(8,128)(2,1)}, bf16[16,14,14,256]{3,0,2,1:T(8,128)(2,1)}, bf16[16,14...) fusion(bf16[16,14,14,256]{3,0,2,1:T(8,128)(2,1)S(1)} %bitcast.89), kind=kLoop, calls=%fused_computation.4 | loop fusion | bytes 14450688 | tf_op jit(solution)/shard_map/slice | solution.py:16
  20.8 1.8 copy.28
  22.7 3.6 reshape.70
  26.3 3.3 copy.30
  29.6 3.6 reshape.71
  33.2 3.3 copy.31
  36.5 3.6 reshape.72
  40.1 3.3 copy.32
  43.3 3.7 reshape.73
  47.0 3.4 convolution_dynamic-update-slice_fusion.7
  54.7 1.5 fusion.25
  56.8 1.4 reshape.74
  58.2 2.0 copy.36
  61.6 2.0 copy.37
  65.0 2.0 copy.38
  67.1 1.4 reshape.77
  68.5 2.3 copy.39
  70.8 1.8 fusion.24
  72.6 2.1 fusion.22
  74.7 2.0 fusion.20
  80.1 2.1 fusion.14
  82.2 2.3 fusion.12
  84.5 2.1 fusion.10
  93.2 172.3 %all-reduce.7.cloned.1.call-done = (f32[2304,256]{1,0:T(8,128)}, f32[2304,256]{1,0:T(8,128)}) async-done(((f32[2304,256]{1,0:T(8,128)}, f32[2304,256]{1,0:T(8,128)}), (f32[2304,256]{1,0:T(8,128)}, f32[2304,256]{1,0:T(8,128)})) %all-reduce.7.cloned.1.call-update) | async-done | bytes 4718608 | tf_op jit(solution)/shard_map/psum | solution.py:56
  268.9 19.3 %psum.44 = f32[2]{0:T(128)S(1)} all-reduce(f32[2]{0:T(128)S(1)} %add_convert_fusion), channel_id=1, replica_groups=mesh['gx'=4,'gy'=8] {'gy'}, use_global_device_ids=true, to_apply=%region_4.5 | all-reduce | flops 2 | bytes 16 | tf_op jit(solution)/shard_map/psum | solution.py:56
  288.2 6.5 %psum.45 = f32[2]{0:T(128)S(1)} all-reduce(f32[2]{0:T(128)S(1)} %psum.44), channel_id=1, replica_groups=mesh['gx'=4,'gy'=8] {'gx'}, use_global_device_ids=true, to_apply=%region_5.6 | all-reduce | flops 2 | bytes 16 | tf_op jit(solution)/shard_map/psum | solution.py:55
  295.3 65.9 %all-reduce.9.cloned.1.call-done = (f32[2304,256]{1,0:T(8,128)}, f32[2304,256]{1,0:T(8,128)}) async-done(((f32[2304,256]{1,0:T(8,128)}, f32[2304,256]{1,0:T(8,128)}), (f32[2304,256]{1,0:T(8,128)}, f32[2304,256]{1,0:T(8,128)})) %all-reduce.9.cloned.1.call-update) | async-done | bytes 4718608 | tf_op jit(solution)/shard_map/psum | solution.py:55
  361.2 10.5 %multiply_subtract_fusion = (f32[2304,256]{1,0:T(8,128)}, f32[2304,256]{1,0:T(8,128)}, f32[2304,256]{1,0:T(8,128)}, f32[2304,256]{1,0:T(8,128)}) fusion(f32[2304,256]{1,0:T(8,128)} %param.17, f32[2304,256]{1,0:T(8,128)} %get-tuple-element.7, f32[]{:T(128)} %bitcast.25, f32[2304,256]{1,0:T(8,128)} %param.19, f32[2304,256]{1,0:T(8,128)} %param.16, ...), kind=kLoop, calls=%fused_computation | loop fusion | flops 5898240 | bytes 23592968 | tf_op jit(solution)/shard_map/sub | solution.py:29
  (54 shorter events, 22.4 us)
Async XLA Ops:
  7.2 63.6 %copy-start = (bf16[2,48,32,256]{3,2,1,0:T(8,128)(2,1)S(1)}, bf16[2,48,32,256]{3,2,1,0:T(8,128)(2,1)}, u32[]{:S(2)}) copy-start(bf16[2,48,32,256]{3,2,1,0:T(8,128)(2,1)} %param.14) | copy-start | bytes 4718596
  7.2 258.4 %all-reduce.7.cloned.1.call-start = ((), (), s32[]{:S(2)}) async-start(), calls=%async_computation | async-start | bytes 9437184 | tf_op jit(solution)/shard_map/psum | solution.py:56
  47.0 3.4 copy-start.5
  47.0 3.4 copy-start.11
  50.4 1.4 copy-start.12
  51.8 1.4 copy-start.13
  53.2 1.4 copy-start.2
  54.7 1.5 copy-start.1
  76.7 1.4 copy-start.3
  84.5 2.1 copy-start.6
  84.5 2.1 copy-start.7
  86.6 1.5 copy-start.4
  86.6 2.4 copy-start.8
  89.0 1.4 copy-start.9
  90.4 1.4 copy-start.10
  93.2 268.0 %all-reduce.9.cloned.1.call-start = ((), (), s32[]{:S(2)}) async-start(), calls=%async_computation.1 | async-start | bytes 9437184 | tf_op jit(solution)/shard_map/psum | solution.py:55
  265.6 0.7 copy-start.14
  265.6 1.3 copy-start.15
Sparse Core Ops, SparseCore 0:
  93.3 172.2 all-reduce.6
  268.0 93.1 all-reduce.8
